TPU v7x, 32 devices: a whole 2x2x4 slice. The times are simulated.
32 devices in a mesh: gx: 4 (over z), gy: 8 (over y, x, core).
Axes of the slice: x: 2, y: 2, z: 4, core: 2. Of those that a mesh axis runs over, the one named last changes fastest.
Arguments:
- tokens: bfloat16 [33856, 768], P(('gx', 'gy')), may hold values from -6 to 6
- lengths: int32 [64], P(('gx', 'gy')), may hold values from 40 to 529, as said below
- key_mask: int32 [64, 529], P(('gx', 'gy')), may hold values 0 or 1
- ln1_gain: bfloat16 [768], P(('gx', 'gy')), may hold values from 0.5 to 1.5
- ln1_bias: bfloat16 [768], P(('gx', 'gy')), may hold values from -1.1953125 to 1.1953125
- q_weight: bfloat16 [768, 768], P(('gx', 'gy')), may hold values from -0.21875 to 0.21875
- q_bias: bfloat16 [768], P(('gx', 'gy')), may hold values from -1.1953125 to 1.1953125
- k_weight: bfloat16 [768, 768], P(('gx', 'gy')), may hold values from -0.21875 to 0.21875
- v_weight: bfloat16 [768, 768], P(('gx', 'gy')), may hold values from -0.21875 to 0.21875
- v_bias: bfloat16 [768], P(('gx', 'gy')), may hold values from -1.1953125 to 1.1953125
- o_weight: bfloat16 [768, 768], P(('gx', 'gy')), may hold values from -3.5 to 3.5
- o_bias: bfloat16 [768], P(('gx', 'gy')), may hold values from -1.1953125 to 1.1953125
- ln2_gain: bfloat16 [768], P(('gx', 'gy')), may hold values from 0.5 to 1.5
- ln2_bias: bfloat16 [768], P(('gx', 'gy')), may hold values from -1.1953125 to 1.1953125
- up_weight: bfloat16 [768, 3072], P(('gx', 'gy')), may hold values from -0.21875 to 0.21875
- up_bias: bfloat16 [3072], P(('gx', 'gy')), may hold values from -1.1953125 to 1.1953125
- down_weight: bfloat16 [3072, 768], P(('gx', 'gy')), may hold values from -0.21875 to 0.21875
- down_bias: bfloat16 [768], P(('gx', 'gy')), may hold values from -1.1953125 to 1.1953125
- out_grad: bfloat16 [33856, 768], P(('gx', 'gy')), may hold values from -6 to 6
Outputs:
- block_out: bfloat16 [33856, 768], P(('gx', 'gy'))
- grad_tokens: float32 [33856, 768], P(('gx', 'gy'))
- grad_ln1_gain: float32 [768], P(('gx', 'gy'))
- grad_ln1_bias: float32 [768], P(('gx', 'gy'))
- grad_q_weight: float32 [768, 768], P(('gx', 'gy'))
- grad_q_bias: float32 [768], P(('gx', 'gy'))
- grad_k_weight: float32 [768, 768], P(('gx', 'gy'))
- grad_v_weight: float32 [768, 768], P(('gx', 'gy'))
- grad_v_bias: float32 [768], P(('gx', 'gy'))
- grad_o_weight: float32 [768, 768], P(('gx', 'gy'))
- grad_o_bias: float32 [768], P(('gx', 'gy'))
- grad_ln2_gain: float32 [768], P(('gx', 'gy'))
- grad_ln2_bias: float32 [768], P(('gx', 'gy'))
- grad_up_weight: float32 [768, 3072], P(('gx', 'gy'))
- grad_up_bias: float32 [3072], P(('gx', 'gy'))
- grad_down_weight: float32 [3072, 768], P(('gx', 'gy'))
- grad_down_bias: float32 [768], P(('gx', 'gy'))
Inputs may be any that keep to these rules, and one draw needn't show every extreme that they name: `lengths`: most strips are nearly full, and strip 0 holds 529 filled slots.
All inputs are finite; a program needn't handle non-finite values. No bound on the sum of `key_mask` on one device may be relied on, other than what follows from the above.
Results may differ from a plain program's by a relative error of at most 0.012.
Values may be sent and summed in bfloat16 or wider, within the bound.
A program may use at most 192 MiB of HBM per device.

v0:
```python
import math
import jax
import jax.numpy as jnp
from jax import lax
from jax.sharding import PartitionSpec as P

HEAD_DIM = 64
EPSILON = 1e-06
NEG_FILL = -1e30


def layer_norm(values, gain_vec, bias_vec):
    center = values - jnp.mean(values, axis=-1, keepdims=True)
    spread = jnp.mean(center * center, axis=-1, keepdims=True)
    return center * lax.rsqrt(spread + EPSILON) * gain_vec + bias_vec


def gelu_exact(values):
    return jax.nn.gelu(values, approximate=False)


def right_mul(left_arg, right_arg):
    return jnp.dot(left_arg, right_arg, preferred_element_type=jnp.float32)


def left_mul(left_arg, right_arg):
    return lax.dot_general(
        left_arg, right_arg, (((0,), (0,)), ((), ())), preferred_element_type=jnp.float32
    )


def back_mul(left_arg, right_arg):
    return lax.dot_general(
        left_arg, right_arg, (((1,), (1,)), ((), ())), preferred_element_type=jnp.float32
    )


def collect(
    ln1_gain,
    ln1_bias,
    q_weight,
    q_bias,
    k_weight,
    v_weight,
    v_bias,
    o_weight,
    o_bias,
    ln2_gain,
    ln2_bias,
    up_weight,
    up_bias,
    down_weight,
    down_bias,
):
    return (
        lax.all_gather(ln1_gain, ("gx", "gy"), axis=0, tiled=True),
        lax.all_gather(ln1_bias, ("gx", "gy"), axis=0, tiled=True),
        lax.all_gather(q_weight, ("gx", "gy"), axis=0, tiled=True),
        lax.all_gather(q_bias, ("gx", "gy"), axis=0, tiled=True),
        lax.all_gather(k_weight, ("gx", "gy"), axis=0, tiled=True),
        lax.all_gather(v_weight, ("gx", "gy"), axis=0, tiled=True),
        lax.all_gather(v_bias, ("gx", "gy"), axis=0, tiled=True),
        lax.all_gather(o_weight, ("gx", "gy"), axis=0, tiled=True),
        lax.all_gather(o_bias, ("gx", "gy"), axis=0, tiled=True),
        lax.all_gather(ln2_gain, ("gx", "gy"), axis=0, tiled=True),
        lax.all_gather(ln2_bias, ("gx", "gy"), axis=0, tiled=True),
        lax.all_gather(up_weight, ("gx", "gy"), axis=0, tiled=True),
        lax.all_gather(up_bias, ("gx", "gy"), axis=0, tiled=True),
        lax.all_gather(down_weight, ("gx", "gy"), axis=0, tiled=True),
        lax.all_gather(down_bias, ("gx", "gy"), axis=0, tiled=True),
    )


def spread_grads(
    grad_g1,
    grad_b1,
    grad_wq,
    grad_bq,
    grad_wk,
    grad_wv,
    grad_bv,
    grad_wo,
    grad_bo,
    grad_g2,
    grad_b2,
    grad_wup,
    grad_bup,
    grad_wdown,
    grad_bdown,
):
    return (
        lax.psum_scatter(grad_g1, ("gx", "gy"), scatter_dimension=0, tiled=True),
        lax.psum_scatter(grad_b1, ("gx", "gy"), scatter_dimension=0, tiled=True),
        lax.psum_scatter(grad_wq, ("gx", "gy"), scatter_dimension=0, tiled=True),
        lax.psum_scatter(grad_bq, ("gx", "gy"), scatter_dimension=0, tiled=True),
        lax.psum_scatter(grad_wk, ("gx", "gy"), scatter_dimension=0, tiled=True),
        lax.psum_scatter(grad_wv, ("gx", "gy"), scatter_dimension=0, tiled=True),
        lax.psum_scatter(grad_bv, ("gx", "gy"), scatter_dimension=0, tiled=True),
        lax.psum_scatter(grad_wo, ("gx", "gy"), scatter_dimension=0, tiled=True),
        lax.psum_scatter(grad_bo, ("gx", "gy"), scatter_dimension=0, tiled=True),
        lax.psum_scatter(grad_g2, ("gx", "gy"), scatter_dimension=0, tiled=True),
        lax.psum_scatter(grad_b2, ("gx", "gy"), scatter_dimension=0, tiled=True),
        lax.psum_scatter(grad_wup, ("gx", "gy"), scatter_dimension=0, tiled=True),
        lax.psum_scatter(grad_bup, ("gx", "gy"), scatter_dimension=0, tiled=True),
        lax.psum_scatter(grad_wdown, ("gx", "gy"), scatter_dimension=0, tiled=True),
        lax.psum_scatter(grad_bdown, ("gx", "gy"), scatter_dimension=0, tiled=True),
    )


def shards(
    tokens,
    lengths,
    key_mask,
    ln1_gain,
    ln1_bias,
    q_weight,
    q_bias,
    k_weight,
    v_weight,
    v_bias,
    o_weight,
    o_bias,
    ln2_gain,
    ln2_bias,
    up_weight,
    up_bias,
    down_weight,
    down_bias,
    out_grad,
):
    gathered = collect(
        ln1_gain,
        ln1_bias,
        q_weight,
        q_bias,
        k_weight,
        v_weight,
        v_bias,
        o_weight,
        o_bias,
        ln2_gain,
        ln2_bias,
        up_weight,
        up_bias,
        down_weight,
        down_bias,
    )
    row_count = tokens.shape[0]
    feature_count = tokens.shape[1]
    strip_count = lengths.shape[0]
    slot_count = row_count // strip_count
    head_count = feature_count // HEAD_DIM
    score_scale = 1.0 / math.sqrt(HEAD_DIM)
    slot_ids = lax.iota(jnp.int32, slot_count)
    visible = (slot_ids[None, :] == 0) | (slot_ids[None, :] < lengths[:, None]) & (key_mask == 1)

    def split_heads(values):
        return values.reshape(strip_count, slot_count, head_count, HEAD_DIM)

    gain_one = gathered[0].astype(jnp.float32)
    bias_one = gathered[1].astype(jnp.float32)
    gain_two = gathered[9].astype(jnp.float32)
    bias_two = gathered[10].astype(jnp.float32)
    inputs = tokens.astype(jnp.float32)
    normed = layer_norm(inputs, gain_one, bias_one).astype(jnp.bfloat16)
    queries = (right_mul(normed, gathered[2]) + gathered[3].astype(jnp.float32)).astype(
        jnp.bfloat16
    )
    key_rows = right_mul(normed, gathered[4]).astype(jnp.bfloat16)
    value_rows = (right_mul(normed, gathered[5]) + gathered[6].astype(jnp.float32)).astype(
        jnp.bfloat16
    )

    def attend(pieces):
        queries_in, keys_in, values_in, visible_in = pieces
        scores = (
            jnp.einsum("qhd,khd->hqk", queries_in, keys_in, preferred_element_type=jnp.float32)
            * score_scale
        )
        scores = jnp.where(visible_in[None, None, :], scores, NEG_FILL)
        row_max = jnp.max(scores, axis=-1, keepdims=True)
        powers = jnp.exp(scores - row_max)
        row_sum = jnp.sum(powers, axis=-1, keepdims=True)
        attn_low = (powers / row_sum).astype(jnp.bfloat16)
        context = jnp.einsum(
            "hqk,khd->qhd", attn_low, values_in, preferred_element_type=jnp.float32
        )
        return (context, row_max + jnp.log(row_sum))

    context, log_sums = lax.map(
        attend, (split_heads(queries), split_heads(key_rows), split_heads(value_rows), visible)
    )
    context = context.reshape(row_count, feature_count).astype(jnp.bfloat16)
    residual = inputs + right_mul(context, gathered[7]) + gathered[8].astype(jnp.float32)
    normed2 = layer_norm(residual, gain_two, bias_two).astype(jnp.bfloat16)
    hidden = right_mul(normed2, gathered[11]) + gathered[12].astype(jnp.float32)
    active = gelu_exact(hidden).astype(jnp.bfloat16)
    mlp_out = right_mul(active, gathered[13]) + gathered[14].astype(jnp.float32)
    block_out = (residual + mlp_out).astype(jnp.bfloat16)
    regathered = collect(
        ln1_gain,
        ln1_bias,
        q_weight,
        q_bias,
        k_weight,
        v_weight,
        v_bias,
        o_weight,
        o_bias,
        ln2_gain,
        ln2_bias,
        up_weight,
        up_bias,
        down_weight,
        down_bias,
    )
    cotangent = out_grad.astype(jnp.float32)
    grad_wdown = left_mul(active, out_grad)
    grad_bdown = jnp.sum(cotangent, axis=0)
    grad_active = back_mul(out_grad, regathered[13])
    _, gelu_pull = jax.vjp(gelu_exact, hidden)
    grad_hidden = gelu_pull(grad_active)[0].astype(jnp.bfloat16)
    grad_wup = left_mul(normed2, grad_hidden)
    grad_bup = jnp.sum(grad_hidden.astype(jnp.float32), axis=0)
    grad_normed2 = back_mul(grad_hidden, regathered[11])
    _, second_pull = jax.vjp(layer_norm, residual, gain_two, bias_two)
    grad_res, grad_g2, grad_b2 = second_pull(grad_normed2)
    grad_res = cotangent + grad_res
    grad_att = grad_res.astype(jnp.bfloat16)
    grad_wo = left_mul(context, grad_att)
    grad_bo = jnp.sum(grad_att.astype(jnp.float32), axis=0)
    grad_context = back_mul(grad_att, regathered[7]).astype(jnp.bfloat16)

    def attend_back(pieces):
        queries_in, keys_in, values_in, visible_in, lse_in, grad_in = pieces
        scores = (
            jnp.einsum("qhd,khd->hqk", queries_in, keys_in, preferred_element_type=jnp.float32)
            * score_scale
        )
        scores = jnp.where(visible_in[None, None, :], scores, NEG_FILL)
        attn_probs = jnp.exp(scores - lse_in)
        attn_low = attn_probs.astype(jnp.bfloat16)
        grad_values = jnp.einsum(
            "hqk,qhd->khd", attn_low, grad_in, preferred_element_type=jnp.float32
        )
        grad_probs = jnp.einsum(
            "qhd,khd->hqk", grad_in, values_in, preferred_element_type=jnp.float32
        )
        row_inner = jnp.sum(attn_probs * grad_probs, axis=-1, keepdims=True)
        grad_scores = (attn_probs * (grad_probs - row_inner)).astype(jnp.bfloat16)
        grad_queries = (
            jnp.einsum("hqk,khd->qhd", grad_scores, keys_in, preferred_element_type=jnp.float32)
            * score_scale
        )
        grad_keys = (
            jnp.einsum("hqk,qhd->khd", grad_scores, queries_in, preferred_element_type=jnp.float32)
            * score_scale
        )
        return (
            grad_queries.astype(jnp.bfloat16),
            grad_keys.astype(jnp.bfloat16),
            grad_values.astype(jnp.bfloat16),
        )

    grad_queries, grad_keys, grad_values = lax.map(
        attend_back,
        (
            split_heads(queries),
            split_heads(key_rows),
            split_heads(value_rows),
            visible,
            log_sums,
            split_heads(grad_context),
        ),
    )
    grad_queries = grad_queries.reshape(row_count, feature_count)
    grad_keys = grad_keys.reshape(row_count, feature_count)
    grad_values = grad_values.reshape(row_count, feature_count)
    grad_wq = left_mul(normed, grad_queries)
    grad_wk = left_mul(normed, grad_keys)
    grad_wv = left_mul(normed, grad_values)
    grad_bq = jnp.sum(grad_queries.astype(jnp.float32), axis=0)
    grad_bv = jnp.sum(grad_values.astype(jnp.float32), axis=0)
    grad_normed = (
        back_mul(grad_queries, regathered[2])
        + back_mul(grad_keys, regathered[4])
        + back_mul(grad_values, regathered[5])
    )
    _, first_pull = jax.vjp(layer_norm, inputs, gain_one, bias_one)
    grad_inputs, grad_g1, grad_b1 = first_pull(grad_normed)
    grad_tokens = grad_res + grad_inputs
    shares = spread_grads(
        grad_g1,
        grad_b1,
        grad_wq,
        grad_bq,
        grad_wk,
        grad_wv,
        grad_bv,
        grad_wo,
        grad_bo,
        grad_g2,
        grad_b2,
        grad_wup,
        grad_bup,
        grad_wdown,
        grad_bdown,
    )
    return (block_out, grad_tokens) + tuple(shares)


def solution(mesh):
    return jax.shard_map(
        shards,
        mesh=mesh,
        in_specs=(
            P(("gx", "gy"), None),
            P(("gx", "gy")),
            P(("gx", "gy"), None),
            P(("gx", "gy")),
            P(("gx", "gy")),
            P(("gx", "gy"), None),
            P(("gx", "gy")),
            P(("gx", "gy"), None),
            P(("gx", "gy"), None),
            P(("gx", "gy")),
            P(("gx", "gy"), None),
            P(("gx", "gy")),
            P(("gx", "gy")),
            P(("gx", "gy")),
            P(("gx", "gy"), None),
            P(("gx", "gy")),
            P(("gx", "gy"), None),
            P(("gx", "gy")),
            P(("gx", "gy"), None),
        ),
        out_specs=(
            P(("gx", "gy"), None),
            P(("gx", "gy"), None),
            P(("gx", "gy")),
            P(("gx", "gy")),
            P(("gx", "gy"), None),
            P(("gx", "gy")),
            P(("gx", "gy"), None),
            P(("gx", "gy"), None),
            P(("gx", "gy")),
            P(("gx", "gy"), None),
            P(("gx", "gy")),
            P(("gx", "gy")),
            P(("gx", "gy")),
            P(("gx", "gy"), None),
            P(("gx", "gy")),
            P(("gx", "gy"), None),
            P(("gx", "gy")),
        ),
        check_vma=False,
    )
```

profile of v0, /device:TPU:0, one launch (start us, length us, event | category | flops | bytes accessed | tf_op | source)
XLA Modules:
  0.0 1127.2 jit_solution(7891332789321585317)
XLA Ops:
  18.9 42.9 %all-reduce.19 = (bf16[768]{0:T(1024)(128)(2,1)S(1)}, bf16[768]{0:T(1024)(128)(2,1)S(1)}, bf16[768]{0:T(1024)(128)(2,1)S(1)}, bf16[768]{0:T(1024)(128)(2,1)S(1)}...) all-reduce(bf16[768]{0:T(1024)(128)(2,1)S(1)} %dynamic-update-slice, ...), channel_id=1, replica_groups=mesh['gx'=4,'gy'=8] {'gx','gy'}, use_global_device_ids=true, to_apply=%add.2 | all-reduce | flops 9216 | bytes 36864
  80.7 43.1 %all-gather.7.cloned.1.call-done = bf16[768,768]{1,0:T(8,128)(2,1)} async-done(((bf16[24,768]{1,0:T(8,128)(2,1)}), bf16[768,768]{1,0:T(8,128)(2,1)}) %all-gather.7.cloned.1.call-update) | async-done | bytes 1179664 | tf_op jit(solution)/shard_map/all_gather | solution.py:61
  140.8 38.7 %all-gather.9.cloned.1.call-done = bf16[768,768]{1,0:T(8,128)(2,1)} async-done(((bf16[24,768]{1,0:T(8,128)(2,1)}), bf16[768,768]{1,0:T(8,128)(2,1)}) %all-gather.9.cloned.1.call-update) | async-done | bytes 1179664 | tf_op jit(solution)/shard_map/all_gather | solution.py:58
  196.8 58.1 %while.26 = (s32[]{:T(128)}, bf16[2,529,12,64]{1,3,2,0:T(8,128)(2,1)}, f32[2,12,529,1]{2,1,3,0:T(8,128)S(1)}, bf16[2,529,12,64]{1,3,2,0:T(8,128)(2,1)}, pred[2,5...) while((s32[]{:T(128)}, ...), condition=%wide.region_5.6_spmd, body=%wide.region_2.5_spmd.sunk | while | flops 899962304 | bytes 54692004 | solution.py:190
  196.8 10.5 fusion.139
  207.4 9.3 fusion.140
  216.7 9.0 bitcast_dynamic-update-slice_fusion.4
  225.7 10.5 fusion.139
  236.3 9.3 fusion.140
  245.6 8.8 bitcast_dynamic-update-slice_fusion.4
  270.1 30.4 %all-gather.15.cloned.1.call-done = bf16[768,3072]{1,0:T(8,128)(2,1)} async-done(((bf16[24,3072]{1,0:T(8,128)(2,1)}), bf16[768,3072]{1,0:T(8,128)(2,1)}) %all-gather.15.cloned.1.call-update) | async-done | bytes 4718608 | tf_op jit(solution)/shard_map/all_gather | solution.py:67
  300.5 38.0 %multiply_convert_fusion.3 = (bf16[1058,3072]{1,0:T(8,128)(2,1)}, f32[1058,3072]{1,0:T(8,128)}, f32[1058,3072]{1,0:T(8,128)}) fusion(f32[3072]{0:T(1024)S(1)} %copy-done.40, bf16[768,3072]{1,0:T(8,128)(2,1)} %all-gather.15.cloned.1.call-done, f32[1058,768]{1,0:T(8,128)S(1)} %get-tuple-element.237, f32[768]{0:T(1024)S(1)} %copy-done.37, ...), kind=kOutput, calls=%fused_computation.61 | convolution fusion | flops 5210844672 | bytes 40497424 | tf_op jit(solution)/shard_map/dot_general | solution.py:23
  338.5 26.7 %all-gather.17.cloned.1.call-done = bf16[3072,768]{1,0:T(8,128)(2,1)} async-done(((bf16[96,768]{1,0:T(8,128)(2,1)}), bf16[3072,768]{1,0:T(8,128)(2,1)}) %all-gather.17.cloned.1.call-update) | async-done | bytes 4718608 | tf_op jit(solution)/shard_map/all_gather | solution.py:69
  365.2 19.3 %convert_reduce_fusion = (f32[3072]{0:T(1024)}, bf16[1058,3072]{1,0:T(8,128)(2,1)}) fusion(f32[1058,3072]{1,0:T(8,128)} %get-tuple-element.229, f32[1058,3072]{1,0:T(8,128)} %get-tuple-element.238, bf16[1058,768]{1,0:T(8,128)(2,1)} %param.41, bf16[3072,768]{1,0:T(8,128)(2,1)} %all-gather.17.cloned.1.call-done), kind=kOutput, calls=%fused_computation.59 | convolution fusion | flops 5044270080 | bytes 38857728 | tf_op jit(solution)/shard_map/dot_general | solution.py:33
  384.5 10.7 multiply_reduce_fusion.1
  416.3 100.3 %while.27 = (s32[]{:T(128)}, bf16[2,529,12,64]{1,3,2,0:T(8,128)(2,1)}, bf16[2,529,12,64]{1,3,2,0:T(8,128)(2,1)}, bf16[2,529,12,64]{1,3,2,0:T(8,128)(2,1)}, bf16[...) while((s32[]{:T(128)}, ...), condition=%wide.region_12.13_spmd, body=%wide.region_10.12_spmd.sunk | while | flops 2181426688 | bytes 142791664 | solution.py:265
  416.4 10.1 fusion.149
  426.5 12.3 %multiply_reduce_fusion.5 = (f32[12,529]{1,0:T(8,128)S(1)}, f32[12,529,529]{1,2,0:T(8,128)}) fusion(f32[12,529,529]{1,2,0:T(8,128)} %fusion.149, f32[12,529]{1,0:T(8,128)S(1)} %dynamic-slice_bitcast_fusion.2, bf16[2,529,12,64]{1,3,2,0:T(8,128)(2,1)S(1)} %get-tuple-element.407, s32[]{:T(128)S(6)} %copy.124, ...), kind=kOutput, calls=%fused_computation.21.clone.1 | convolution fusion | flops 446619840 | bytes 28899216 | tf_op jit(solution)/shard_map/while/body/eval_jaxpr/qhd,khd->hqk/dot_general | solution.py:237
  438.8 11.6 %multiply_convert_fusion.5 = bf16[12,529,529]{1,2,0:T(8,128)(2,1)S(1)} fusion(f32[12,529,529]{1,2,0:T(8,128)} %get-tuple-element.355, f32[12,529,529]{1,2,0:T(8,128)} %fusion.149, f32[12,529]{1,0:T(8,128)S(1)} %get-tuple-element.356), kind=kLoop, calls=%fused_computation.20.clone.1 | loop fusion | flops 10074276 | bytes 33606312 | tf_op jit(solution)/shard_map/while/body/eval_jaxpr/convert_element_type | solution.py:250
  450.5 9.4 fusion.152
  466.6 10.1 fusion.149
  476.7 12.3 %multiply_reduce_fusion.5 = (f32[12,529]{1,0:T(8,128)S(1)}, f32[12,529,529]{1,2,0:T(8,128)}) fusion(f32[12,529,529]{1,2,0:T(8,128)} %fusion.149, f32[12,529]{1,0:T(8,128)S(1)} %dynamic-slice_bitcast_fusion.2, bf16[2,529,12,64]{1,3,2,0:T(8,128)(2,1)S(1)} %get-tuple-element.407, s32[]{:T(128)S(6)} %copy.124, ...), kind=kOutput, calls=%fused_computation.21.clone.1 | convolution fusion | flops 446619840 | bytes 28899216 | tf_op jit(solution)/shard_map/while/body/eval_jaxpr/qhd,khd->hqk/dot_general | solution.py:237
  489.0 11.4 %multiply_convert_fusion.5 = bf16[12,529,529]{1,2,0:T(8,128)(2,1)S(1)} fusion(f32[12,529,529]{1,2,0:T(8,128)} %get-tuple-element.355, f32[12,529,529]{1,2,0:T(8,128)} %fusion.149, f32[12,529]{1,0:T(8,128)S(1)} %get-tuple-element.356), kind=kLoop, calls=%fused_computation.20.clone.1 | loop fusion | flops 10074276 | bytes 33606312 | tf_op jit(solution)/shard_map/while/body/eval_jaxpr/convert_element_type | solution.py:250
  500.4 9.3 fusion.152
  560.3 12.6 %fusion.75 = f32[768,3072]{1,0:T(8,128)} fusion(bf16[1058,3072]{1,0:T(8,128)(2,1)} %get-tuple-element.242, f32[1058,768]{1,0:T(8,128)} %copy-done.6, f32[768]{0:T(1024)S(1)} %copy-done.38, f32[768]{0:T(1024)S(1)} %copy-done.28, f32[1058]{0:T(1024)S(1)} %copy-done.26, f32[1058]{0:T(1024)S(1)} %copy-done.22), kind=kOutput, calls=%fused_computation.127 | convolution fusion | flops 4996333056 | bytes 19202320 | tf_op jit(solution)/shard_map/dot_general | solution.py:27
  573.2 11.2 fusion.92
  601.2 40.1 %all-reduce.18 = (f32[768]{0:T(1024)S(1)}, f32[768]{0:T(1024)S(1)}, f32[768]{0:T(1024)S(1)}, f32[768]{0:T(1024)S(1)}, f32[768]{0:T(1024)S(1)}, /*index=5*/f32[76...) all-reduce(f32[768]{0:T(1024)S(1)} %get-tuple-element.167, ...), channel_id=2, replica_groups=mesh['gx'=4,'gy'=8] {'gx','gy'}, use_global_device_ids=true, to_apply=%region_16.17.clone | all-reduce | flops 9216 | bytes 73728
  646.5 10.3 fusion.63
  656.8 75.6 %reduce-scatter.9.cloned.1.call-done = f32[24,768]{1,0:T(8,128)} async-done(((f32[768,768]{1,0:T(8,128)}), f32[24,768]{1,0:T(8,128)}) %reduce-scatter.9.cloned.1.call-update) | async-done | bytes 73744 | tf_op jit(solution)/shard_map/reduce_scatter | solution.py:96
  732.4 104.4 %reduce-scatter.7.cloned.1.call-done = f32[24,768]{1,0:T(8,128)} async-done(((f32[768,768]{1,0:T(8,128)}), f32[24,768]{1,0:T(8,128)}) %reduce-scatter.7.cloned.1.call-update) | async-done | bytes 73744 | tf_op jit(solution)/shard_map/reduce_scatter | solution.py:94
  836.8 141.6 %reduce-scatter.15.cloned.1.call-done = f32[24,3072]{1,0:T(8,128)} async-done(((f32[768,3072]{1,0:T(8,128)}), f32[24,3072]{1,0:T(8,128)}) %reduce-scatter.15.cloned.1.call-update) | async-done | bytes 294928 | tf_op jit(solution)/shard_map/reduce_scatter | solution.py:103
  978.4 141.4 %reduce-scatter.17.cloned.1.call-done = f32[96,768]{1,0:T(8,128)} async-done(((f32[3072,768]{1,0:T(8,128)}), f32[96,768]{1,0:T(8,128)}) %reduce-scatter.17.cloned.1.call-update) | async-done | bytes 294928 | tf_op jit(solution)/shard_map/reduce_scatter | solution.py:105
  (241 shorter events, 180.0 us)
Async XLA Ops:
  7.2 58.1 %copy-start.4 = (bf16[1058,768]{1,0:T(8,128)(2,1)S(1)}, bf16[1058,768]{1,0:T(8,128)(2,1)}, u32[]{:S(2)}) copy-start(bf16[1058,768]{1,0:T(8,128)(2,1)} %param.23) | copy-start | bytes 4875268
  7.2 59.4 %copy-start.42 = (s32[2,529]{1,0:T(2,128)S(1)}, s32[2,529]{1,0:T(2,128)}, u32[]{:S(2)}) copy-start(s32[2,529]{1,0:T(2,128)} %param.25) | copy-start | bytes 12700
  7.2 59.4 %copy-start.49 = (s32[2]{0:T(128)S(1)}, s32[2]{0:T(128)}, u32[]{:S(2)}) copy-start(s32[2]{0:T(128)} %param.24) | copy-start | bytes 28
  7.2 60.6 %all-gather.11.cloned.1.call-start = ((), (), s32[]{:S(2)}) async-start(), calls=%async_computation.8 | async-start | bytes 1216512 | tf_op jit(solution)/shard_map/all_gather | solution.py:60
  8.0 115.9 %all-gather.7.cloned.1.call-start = ((), (), s32[]{:S(2)}) async-start(), calls=%async_computation.6 | async-start | bytes 1216512 | tf_op jit(solution)/shard_map/all_gather | solution.py:61
  8.7 170.9 %all-gather.9.cloned.1.call-start = ((), (), s32[]{:S(2)}) async-start(), calls=%async_computation.7 | async-start | bytes 1216512 | tf_op jit(solution)/shard_map/all_gather | solution.py:58
  9.4 256.0 %all-gather.13.cloned.1.call-start = ((), (), s32[]{:S(2)}) async-start(), calls=%async_computation.9 | async-start | bytes 1216512 | tf_op jit(solution)/shard_map/all_gather | solution.py:63
  10.0 290.5 %all-gather.15.cloned.1.call-start = ((), (), s32[]{:S(2)}) async-start(), calls=%async_computation.10 | async-start | bytes 4866048 | tf_op jit(solution)/shard_map/all_gather | solution.py:67
  10.6 354.6 %all-gather.17.cloned.1.call-start = ((), (), s32[]{:S(2)}) async-start(), calls=%async_computation.11 | async-start | bytes 4866048 | tf_op jit(solution)/shard_map/all_gather | solution.py:69
  11.2 645.6 %reduce-scatter.13.cloned.1.call-start = ((), (), s32[]{:S(2)}) async-start(), calls=%async_computation.15 | async-start | bytes 2433024 | tf_op jit(solution)/shard_map/reduce_scatter | solution.py:99
  61.7 117.8 %copy-start.35 = (f32[768]{0:T(1024)}, f32[768]{0:T(1024)S(1)}, u32[]{:S(2)}) copy-start(f32[768]{0:T(1024)S(1)} %convert_element_type.111) | copy-start | bytes 9220
  61.7 117.8 %copy-start.43 = (f32[768]{0:T(1024)}, f32[768]{0:T(1024)S(1)}, u32[]{:S(2)}) copy-start(f32[768]{0:T(1024)S(1)} %convert_element_type.112) | copy-start | bytes 9220
  65.3 114.3 %copy-start.23 = (f32[1058]{0:T(1024)}, f32[1058]{0:T(1024)S(1)}, u32[]{:S(2)}) copy-start(f32[1058]{0:T(1024)S(1)} %broadcast_multiply_fusion.1) | copy-start | bytes 12700
  65.9 113.7 %copy-start.29 = (f32[1058]{0:T(1024)}, f32[1058]{0:T(1024)S(1)}, u32[]{:S(2)}) copy-start(f32[1058]{0:T(1024)S(1)} %fusion.72) | copy-start | bytes 12700
  254.9 10.5 copy-start
  254.9 10.5 copy-start.17
  254.9 10.5 copy-start.19
  254.9 10.5 copy-start.45
  269.5 125.7 %copy-start.6 = (f32[1058,768]{1,0:T(8,128)}, f32[1058,768]{1,0:T(8,128)S(1)}, u32[]{:S(2)}) copy-start(f32[1058,768]{1,0:T(8,128)S(1)} %get-tuple-element.237) | copy-start | bytes 9750532
  269.5 31.0 %copy-start.27 = (f32[768]{0:T(1024)S(1)}, f32[768]{0:T(1024)}, u32[]{:S(2)}) copy-start(f32[768]{0:T(1024)} %convert_element_type.122) | copy-start | bytes 9220
  269.5 31.0 %copy-start.37 = (f32[768]{0:T(1024)S(1)}, f32[768]{0:T(1024)}, u32[]{:S(2)}) copy-start(f32[768]{0:T(1024)} %convert_element_type.123) | copy-start | bytes 9220
  269.5 31.0 %copy-start.40 = (f32[3072]{0:T(1024)S(1)}, f32[3072]{0:T(1024)}, u32[]{:S(2)}) copy-start(f32[3072]{0:T(1024)} %convert_element_type.125) | copy-start | bytes 36868
  269.6 125.7 %copy-start.21 = (f32[1058]{0:T(1024)}, f32[1058]{0:T(1024)S(1)}, u32[]{:S(2)}) copy-start(f32[1058]{0:T(1024)S(1)} %broadcast_multiply_fusion) | copy-start | bytes 12700
  270.1 125.1 %copy-start.25 = (f32[1058]{0:T(1024)}, f32[1058]{0:T(1024)S(1)}, u32[]{:S(2)}) copy-start(f32[1058]{0:T(1024)S(1)} %fusion.73) | copy-start | bytes 12700
  402.2 254.6 %reduce-scatter.11.cloned.1.call-start = ((), (), s32[]{:S(2)}) async-start(), calls=%async_computation.14 | async-start | bytes 2433024 | tf_op jit(solution)/shard_map/reduce_scatter | solution.py:97
  416.4 10.1 copy-start.2
  438.8 11.7 %copy-start.3 = (bf16[2,529,12,64]{1,3,2,0:T(8,128)(2,1)S(1)}, bf16[2,529,12,64]{1,3,2,0:T(8,128)(2,1)}, u32[]{:S(2)}) copy-start(bf16[2,529,12,64]{1,3,2,0:T(8,128)(2,1)} %get-tuple-element.411) | copy-start | bytes 4875268 | tf_op jit(solution)/shard_map/while
  489.0 11.4 %copy-start.3 = (bf16[2,529,12,64]{1,3,2,0:T(8,128)(2,1)S(1)}, bf16[2,529,12,64]{1,3,2,0:T(8,128)(2,1)}, u32[]{:S(2)}) copy-start(bf16[2,529,12,64]{1,3,2,0:T(8,128)(2,1)} %get-tuple-element.411) | copy-start | bytes 4875268 | tf_op jit(solution)/shard_map/while
  529.5 202.9 %reduce-scatter.9.cloned.1.call-start = ((), (), s32[]{:S(2)}) async-start(), calls=%async_computation.13 | async-start | bytes 2433024 | tf_op jit(solution)/shard_map/reduce_scatter | solution.py:96
  544.7 292.1 %reduce-scatter.7.cloned.1.call-start = ((), (), s32[]{:S(2)}) async-start(), calls=%async_computation.12 | async-start | bytes 2433024 | tf_op jit(solution)/shard_map/reduce_scatter | solution.py:94
  560.2 418.1 %reduce-scatter.15.cloned.1.call-start = ((), (), s32[]{:S(2)}) async-start(), calls=%async_computation.16 | async-start | bytes 9732096 | tf_op jit(solution)/shard_map/reduce_scatter | solution.py:103
  572.9 546.9 %reduce-scatter.17.cloned.1.call-start = ((), (), s32[]{:S(2)}) async-start(), calls=%async_computation.17 | async-start | bytes 9732096 | tf_op jit(solution)/shard_map/reduce_scatter | solution.py:105
  (36 other events, 163.6 us)
Sparse Core Ops, SparseCore 0:
  10.9 56.8 all-gather.10
  70.7 53.0 all-gather.6
  126.7 52.8 all-gather.8
  182.3 52.8 all-gather.12
  237.9 62.4 all-gather.14
  303.2 61.9 all-gather.16
  402.3 97.9 reduce-scatter.12
  529.6 98.0 reduce-scatter.10
  633.6 98.7 reduce-scatter.8
  738.1 98.6 reduce-scatter.6
  843.2 135.1 reduce-scatter.14
  984.7 135.0 reduce-scatter.16
where the time goes:
time: 1130 us
  waiting for transfers between devices  607 us (54%)
  matrix products  260 us (23%)
  local copies, waits for them, and re-layouts  103 us (9%)
  blocking collectives  82.9 us (7%)
  other arithmetic  56.9 us (5%)
  between operations  15.4 us (1%)
    reduce_scatter x1, waiting for transfers between devices, spread_grads(): lax.psum_scatter(grad_wup, ('gx', 'gy'), scatter_dimension=0, tiled=True)  142 us
    reduce_scatter x1, waiting for transfers between devices, spread_grads(): lax.psum_scatter(grad_wdown, ('gx', 'gy'), scatter_dimension=0, tiled=True)  141 us
    reduce_scatter x1, waiting for transfers between devices, spread_grads(): lax.psum_scatter(grad_wq, ('gx', 'gy'), scatter_dimension=0, tiled=True)  104 us
    unnamed x2, blocking collectives  82.9 us
    reduce_scatter x1, waiting for transfers between devices, spread_grads(): lax.psum_scatter(grad_wk, ('gx', 'gy'), scatter_dimension=0, tiled=True)  75.6 us
    dot_general x6, matrix products, right_mul(): return jnp.dot(left_arg, right_arg, preferred_element_type=jnp.float32)  64.8 us
    all_gather x1, waiting for transfers between devices, collect(): lax.all_gather(v_weight, ('gx', 'gy'), axis=0, tiled=True)  43.1 us
    dot_general x6, matrix products, left_mul(): lax.dot_general(left_arg, right_arg, (((0,), (0,)), ((), ())), preferred_...  41.3 us
  transfers between devices with their start and end apart: 12, of which 9 were waited for; matrix products, arithmetic and copies ran while one was open for 34% of the time, Pallas kernels for 0%

commit v1 on v0

--- a/solution.py
+++ b/solution.py
@@ -52,13 +52,32 @@
     down_weight,
     down_bias,
 ):
+
+    def note_matrix(mat):
+        named_axis = ("gx", "gy")
+        left_arr, y_new, built = (
+            jax.lax.axis_size(named_axis),
+            jax.lax.axis_index(named_axis),
+            mat.shape[0],
+        )
+        taken_in, tmp = (mat, 1)
+        while tmp < left_arr:
+            xs_all = []
+            for h in range(left_arr):
+                xs_all.append((h, (h - tmp) % left_arr))
+            taken_in = jnp.concatenate(
+                [taken_in, jax.lax.ppermute(taken_in, axis_name=named_axis, perm=xs_all)], 0
+            )
+            tmp = 2 * tmp
+        return jnp.roll(taken_in, y_new * built, 0)
+
     return (
         lax.all_gather(ln1_gain, ("gx", "gy"), axis=0, tiled=True),
         lax.all_gather(ln1_bias, ("gx", "gy"), axis=0, tiled=True),
         lax.all_gather(q_weight, ("gx", "gy"), axis=0, tiled=True),
         lax.all_gather(q_bias, ("gx", "gy"), axis=0, tiled=True),
         lax.all_gather(k_weight, ("gx", "gy"), axis=0, tiled=True),
-        lax.all_gather(v_weight, ("gx", "gy"), axis=0, tiled=True),
+        note_matrix(v_weight),
         lax.all_gather(v_bias, ("gx", "gy"), axis=0, tiled=True),
         lax.all_gather(o_weight, ("gx", "gy"), axis=0, tiled=True),
         lax.all_gather(o_bias, ("gx", "gy"), axis=0, tiled=True),

time: 1130 us -> 1100 us (0.973)
  waiting for transfers between devices: 607 us -> 559 us
  starting transfers between devices: 1.34 us -> 13.2 us
    all_gather x1 -> x0, waiting for transfers between devices: 43.1 us -> none  [collect(): lax.all_gather(v_weight, ('gx', 'gy'), axis=0, tiled=True)]
    all_gather x1, waiting for transfers between devices: 38.7 us -> 0.02 us  [collect(): lax.all_gather(q_weight, ('gx', 'gy'), axis=0, tiled=True)]
    ppermute x0 -> x5, waiting for transfers between devices: none -> 37.3 us  [note_matrix(): jax.lax.ppermute(taken_in, axis_name=named_axis, perm=xs_all)]
    ppermute x0 -> x5, starting transfers between devices: none -> 11.9 us  [note_matrix(): jax.lax.ppermute(taken_in, axis_name=named_axis, perm=xs_all)]
  transfers between devices with their start and end apart: 12 -> 16, of which waited for: 9 -> 10; matrix products, arithmetic and copies ran while one was open for 34% -> 34% of each run, Pallas kernels for 0% -> 0%
where the time goes in v1:
time: 1100 us; the launch traced here: 1090 us
  waiting for transfers between devices  559 us (51%)
  matrix products  256 us (23%)
  local copies, waits for them, and re-layouts  99.8 us (9%)
  blocking collectives  83.4 us (8%)
  other arithmetic  59.6 us (5%)
  between operations  15.1 us (1%)
  starting transfers between devices  13.2 us (1%)
    reduce_scatter x1, waiting for transfers between devices, spread_grads(): lax.psum_scatter(grad_wup, ('gx', 'gy'), scatter_dimension=0, tiled=True)  142 us
    reduce_scatter x1, waiting for transfers between devices, spread_grads(): lax.psum_scatter(grad_wdown, ('gx', 'gy'), scatter_dimension=0, tiled=True)  142 us
    reduce_scatter x1, waiting for transfers between devices, spread_grads(): lax.psum_scatter(grad_wq, ('gx', 'gy'), scatter_dimension=0, tiled=True)  105 us
    unnamed x2, blocking collectives  83.4 us
    reduce_scatter x1, waiting for transfers between devices, spread_grads(): lax.psum_scatter(grad_wk, ('gx', 'gy'), scatter_dimension=0, tiled=True)  80.8 us
    dot_general x6, matrix products, right_mul(): return jnp.dot(left_arg, right_arg, preferred_element_type=jnp.float32)  62.2 us
    dot_general x6, matrix products, back_mul(): lax.dot_general(left_arg, right_arg, (((1,), (1,)), ((), ())), preferred_...  40.7 us
    dot_general x6, matrix products, left_mul(): lax.dot_general(left_arg, right_arg, (((0,), (0,)), ((), ())), preferred_...  40 us
  transfers between devices with their start and end apart: 16, of which 10 were waited for; matrix products, arithmetic and copies ran while one was open for 34% of the time, Pallas kernels for 0%

profile of v1, /device:TPU:0, one launch (start us, length us, event | category | flops | bytes accessed | tf_op | source)
XLA Modules:
  0.0 1086.9 jit_solution(730299916113973539)
XLA Ops:
  32.5 43.6 %all-reduce.19 = (bf16[768]{0:T(1024)(128)(2,1)S(1)}, bf16[768]{0:T(1024)(128)(2,1)S(1)}, bf16[768]{0:T(1024)(128)(2,1)S(1)}, bf16[768]{0:T(1024)(128)(2,1)S(1)}...) all-reduce(bf16[768]{0:T(1024)(128)(2,1)S(1)} %dynamic-update-slice, ...), channel_id=1, replica_groups=mesh['gx'=4,'gy'=8] {'gx','gy'}, use_global_device_ids=true, to_apply=%add.2 | all-reduce | flops 9216 | bytes 36864
  82.3 7.5 collective-permute-done.3
  92.4 26.2 %collective-permute-done.4 = bf16[384,768]{1,0:T(8,128)(2,1)S(1)} collective-permute-done((bf16[384,768]{1,0:T(8,128)(2,1)S(1)}, bf16[384,768]{1,0:T(8,128)(2,1)S(1)}, u32[]{:S(2)}, u32[]{:S(2)}) %collective-permute-start.4) | collective-permute-done | bytes 589856 | tf_op jit(solution)/shard_map/ppermute | solution.py:69
  163.1 58.0 %while.26 = (s32[]{:T(128)}, bf16[2,529,12,64]{1,3,2,0:T(8,128)(2,1)}, f32[2,12,529,1]{2,1,3,0:T(8,128)S(1)}, bf16[2,529,12,64]{1,3,2,0:T(8,128)(2,1)}, pred[2,5...) while((s32[]{:T(128)}, ...), condition=%wide.region_5.7_spmd, body=%wide.region_2.6_spmd.sunk | while | flops 899962304 | bytes 54692004 | solution.py:209
  163.5 10.5 fusion.140
  174.1 9.3 fusion.141
  183.4 8.8 bitcast_dynamic-update-slice_fusion.4
  192.3 10.6 fusion.140
  202.8 9.5 fusion.141
  212.3 8.8 bitcast_dynamic-update-slice_fusion.4
  236.5 23.3 %all-gather.12.cloned.1.call-done = bf16[768,3072]{1,0:T(8,128)(2,1)} async-done(((bf16[24,3072]{1,0:T(8,128)(2,1)}), bf16[768,3072]{1,0:T(8,128)(2,1)}) %all-gather.12.cloned.1.call-update) | async-done | bytes 4718608 | tf_op jit(solution)/shard_map/all_gather | solution.py:86
  259.9 38.1 %multiply_convert_fusion.3 = (bf16[1058,3072]{1,0:T(8,128)(2,1)}, f32[1058,3072]{1,0:T(8,128)}, f32[1058,3072]{1,0:T(8,128)}) fusion(f32[3072]{0:T(1024)S(1)} %copy-done.44, bf16[768,3072]{1,0:T(8,128)(2,1)} %all-gather.12.cloned.1.call-done, f32[1058,768]{1,0:T(8,128)S(1)} %get-tuple-element.248, f32[768]{0:T(1024)S(1)} %copy-done.39, ...), kind=kOutput, calls=%fused_computation.61 | convolution fusion | flops 5210844672 | bytes 40497424 | tf_op jit(solution)/shard_map/dot_general | solution.py:23
  298.0 26.6 %all-gather.14.cloned.1.call-done = bf16[3072,768]{1,0:T(8,128)(2,1)} async-done(((bf16[96,768]{1,0:T(8,128)(2,1)}), bf16[3072,768]{1,0:T(8,128)(2,1)}) %all-gather.14.cloned.1.call-update) | async-done | bytes 4718608 | tf_op jit(solution)/shard_map/all_gather | solution.py:88
  324.6 19.3 %convert_reduce_fusion = (f32[3072]{0:T(1024)}, bf16[1058,3072]{1,0:T(8,128)(2,1)}) fusion(f32[1058,3072]{1,0:T(8,128)} %get-tuple-element.230, f32[1058,3072]{1,0:T(8,128)} %get-tuple-element.249, bf16[1058,768]{1,0:T(8,128)(2,1)} %param.43, bf16[3072,768]{1,0:T(8,128)(2,1)} %all-gather.14.cloned.1.call-done), kind=kOutput, calls=%fused_computation.59 | convolution fusion | flops 5044270080 | bytes 38857728 | tf_op jit(solution)/shard_map/dot_general | solution.py:33
  343.8 10.7 multiply_reduce_fusion.1
  375.7 100.4 %while.27 = (s32[]{:T(128)}, bf16[2,529,12,64]{1,3,2,0:T(8,128)(2,1)}, bf16[2,529,12,64]{1,3,2,0:T(8,128)(2,1)}, bf16[2,529,12,64]{1,3,2,0:T(8,128)(2,1)}, bf16[...) while((s32[]{:T(128)}, ...), condition=%wide.region_12.14_spmd, body=%wide.region_10.13_spmd.sunk | while | flops 2181426688 | bytes 142791664 | solution.py:284
  375.8 10.1 fusion.150
  385.9 12.3 %multiply_reduce_fusion.5 = (f32[12,529]{1,0:T(8,128)S(1)}, f32[12,529,529]{1,2,0:T(8,128)}) fusion(f32[12,529,529]{1,2,0:T(8,128)} %fusion.150, f32[12,529]{1,0:T(8,128)S(1)} %dynamic-slice_bitcast_fusion.2, bf16[2,529,12,64]{1,3,2,0:T(8,128)(2,1)S(1)} %get-tuple-element.418, s32[]{:T(128)S(6)} %copy.133, ...), kind=kOutput, calls=%fused_computation.21.clone.1 | convolution fusion | flops 446619840 | bytes 28899216 | tf_op jit(solution)/shard_map/while/body/eval_jaxpr/qhd,khd->hqk/dot_general | solution.py:256
  398.2 11.6 %multiply_convert_fusion.5 = bf16[12,529,529]{1,2,0:T(8,128)(2,1)S(1)} fusion(f32[12,529,529]{1,2,0:T(8,128)} %get-tuple-element.366, f32[12,529,529]{1,2,0:T(8,128)} %fusion.150, f32[12,529]{1,0:T(8,128)S(1)} %get-tuple-element.367), kind=kLoop, calls=%fused_computation.20.clone.1 | loop fusion | flops 10074276 | bytes 33606312 | tf_op jit(solution)/shard_map/while/body/eval_jaxpr/convert_element_type | solution.py:269
  409.9 9.4 fusion.153
  426.1 10.1 fusion.150
  436.1 12.3 %multiply_reduce_fusion.5 = (f32[12,529]{1,0:T(8,128)S(1)}, f32[12,529,529]{1,2,0:T(8,128)}) fusion(f32[12,529,529]{1,2,0:T(8,128)} %fusion.150, f32[12,529]{1,0:T(8,128)S(1)} %dynamic-slice_bitcast_fusion.2, bf16[2,529,12,64]{1,3,2,0:T(8,128)(2,1)S(1)} %get-tuple-element.418, s32[]{:T(128)S(6)} %copy.133, ...), kind=kOutput, calls=%fused_computation.21.clone.1 | convolution fusion | flops 446619840 | bytes 28899216 | tf_op jit(solution)/shard_map/while/body/eval_jaxpr/qhd,khd->hqk/dot_general | solution.py:256
  448.4 11.4 %multiply_convert_fusion.5 = bf16[12,529,529]{1,2,0:T(8,128)(2,1)S(1)} fusion(f32[12,529,529]{1,2,0:T(8,128)} %get-tuple-element.366, f32[12,529,529]{1,2,0:T(8,128)} %fusion.150, f32[12,529]{1,0:T(8,128)S(1)} %get-tuple-element.367), kind=kLoop, calls=%fused_computation.20.clone.1 | loop fusion | flops 10074276 | bytes 33606312 | tf_op jit(solution)/shard_map/while/body/eval_jaxpr/convert_element_type | solution.py:269
  459.9 9.3 fusion.153
  514.5 12.1 %fusion.78 = f32[768,3072]{1,0:T(8,128)} fusion(bf16[1058,3072]{1,0:T(8,128)(2,1)} %get-tuple-element.253, f32[1058,768]{1,0:T(8,128)S(1)} %copy-done.5, f32[768]{0:T(1024)S(1)} %copy-done.40, f32[768]{0:T(1024)S(1)} %copy-done.32, f32[1058]{0:T(1024)S(1)} %copy-done.28, f32[1058]{0:T(1024)S(1)} %copy-done.26), kind=kOutput, calls=%fused_computation.144 | convolution fusion | flops 4996333056 | bytes 19202320 | tf_op jit(solution)/shard_map/dot_general | solution.py:27
  526.9 11.2 %fusion.95 = f32[3072,768]{1,0:T(8,128)} fusion(bf16[1058,3072]{1,0:T(8,128)(2,1)} %get-tuple-element.229, bf16[1058,768]{1,0:T(8,128)(2,1)} %param.43), kind=kOutput, calls=%fused_computation.153 | convolution fusion | flops 4992270336 | bytes 17562624 | tf_op jit(solution)/shard_map/dot_general | solution.py:27
  556.0 39.8 %all-reduce.18 = (f32[768]{0:T(1024)S(1)}, f32[768]{0:T(1024)S(1)}, f32[768]{0:T(1024)S(1)}, f32[768]{0:T(1024)S(1)}, f32[768]{0:T(1024)S(1)}, /*index=5*/f32[76...) all-reduce(f32[768]{0:T(1024)S(1)} %get-tuple-element.168, ...), channel_id=2, replica_groups=mesh['gx'=4,'gy'=8] {'gx','gy'}, use_global_device_ids=true, to_apply=%region_16.18.clone | all-reduce | flops 9216 | bytes 73728
  601.1 9.8 fusion.63
  610.9 80.8 %reduce-scatter.9.cloned.1.call-done = f32[24,768]{1,0:T(8,128)} async-done(((f32[768,768]{1,0:T(8,128)}), f32[24,768]{1,0:T(8,128)}) %reduce-scatter.9.cloned.1.call-update) | async-done | bytes 73744 | tf_op jit(solution)/shard_map/reduce_scatter | solution.py:115
  691.7 104.6 %reduce-scatter.7.cloned.1.call-done = f32[24,768]{1,0:T(8,128)} async-done(((f32[768,768]{1,0:T(8,128)}), f32[24,768]{1,0:T(8,128)}) %reduce-scatter.7.cloned.1.call-update) | async-done | bytes 73744 | tf_op jit(solution)/shard_map/reduce_scatter | solution.py:113
  796.4 141.8 %reduce-scatter.15.cloned.1.call-done = f32[24,3072]{1,0:T(8,128)} async-done(((f32[768,3072]{1,0:T(8,128)}), f32[24,3072]{1,0:T(8,128)}) %reduce-scatter.15.cloned.1.call-update) | async-done | bytes 294928 | tf_op jit(solution)/shard_map/reduce_scatter | solution.py:122
  938.2 141.7 %reduce-scatter.17.cloned.1.call-done = f32[96,768]{1,0:T(8,128)} async-done(((f32[3072,768]{1,0:T(8,128)}), f32[96,768]{1,0:T(8,128)}) %reduce-scatter.17.cloned.1.call-update) | async-done | bytes 294928 | tf_op jit(solution)/shard_map/reduce_scatter | solution.py:124
  (269 shorter events, 189.9 us)
Async XLA Ops:
  7.2 84.5 %copy-start.8 = (bf16[1058,768]{1,0:T(8,128)(2,1)S(1)}, bf16[1058,768]{1,0:T(8,128)(2,1)}, u32[]{:S(2)}) copy-start(bf16[1058,768]{1,0:T(8,128)(2,1)} %param.25) | copy-start | bytes 4875268
  7.2 84.4 %copy-start.46 = (s32[2,529]{1,0:T(2,128)S(1)}, s32[2,529]{1,0:T(2,128)}, u32[]{:S(2)}) copy-start(s32[2,529]{1,0:T(2,128)} %param.27) | copy-start | bytes 12700
  7.2 84.4 %copy-start.55 = (s32[2]{0:T(128)S(1)}, s32[2]{0:T(128)}, u32[]{:S(2)}) copy-start(s32[2]{0:T(128)} %param.26) | copy-start | bytes 28
  7.2 125.9 %all-gather.8.cloned.1.call-start = ((), (), s32[]{:S(2)}) async-start(), calls=%async_computation.7 | async-start | bytes 1216512 | tf_op jit(solution)/shard_map/all_gather | solution.py:79
  8.0 138.1 %all-gather.6.cloned.1.call-start = ((), (), s32[]{:S(2)}) async-start(), calls=%async_computation.6 | async-start | bytes 1216512 | tf_op jit(solution)/shard_map/all_gather | solution.py:77
  8.7 223.2 %all-gather.10.cloned.1.call-start = ((), (), s32[]{:S(2)}) async-start(), calls=%async_computation.8 | async-start | bytes 1216512 | tf_op jit(solution)/shard_map/all_gather | solution.py:82
  9.4 250.4 %all-gather.12.cloned.1.call-start = ((), (), s32[]{:S(2)}) async-start(), calls=%async_computation.9 | async-start | bytes 4866048 | tf_op jit(solution)/shard_map/all_gather | solution.py:86
  10.0 314.5 %all-gather.14.cloned.1.call-start = ((), (), s32[]{:S(2)}) async-start(), calls=%async_computation.10 | async-start | bytes 4866048 | tf_op jit(solution)/shard_map/all_gather | solution.py:88
  10.1 8.4 collective-permute-start
  16.5 594.4 %reduce-scatter.13.cloned.1.call-start = ((), (), s32[]{:S(2)}) async-start(), calls=%async_computation.14 | async-start | bytes 2433024 | tf_op jit(solution)/shard_map/reduce_scatter | solution.py:118
  19.2 4.4 collective-permute-start.1
  20.1 126.0 %copy-start.29 = (f32[1058]{0:T(1024)}, f32[1058]{0:T(1024)S(1)}, u32[]{:S(2)}) copy-start(f32[1058]{0:T(1024)S(1)} %broadcast_multiply_fusion.1) | copy-start | bytes 12700
  24.4 55.0 %collective-permute-start.2 = (bf16[96,768]{1,0:T(8,128)(2,1)S(1)}, bf16[96,768]{1,0:T(8,128)(2,1)S(1)}, u32[]{:S(2)}, u32[]{:S(2)}) collective-permute-start(bf16[96,768]{1,0:T(8,128)(2,1)S(1)} %pad_maximum_fusion.1), channel_id=1, source_target_pairs={{0,28},{1,29},{2,30},{3,31},{4,0},{5,1},{6,2},{7,3},{8,4},{9,5},{1... | collective-permute-start | bytes 442376 | tf_op jit(solution)/shard_map/ppermute | solution.py:69
  76.1 70.0 %copy-start.41 = (f32[768]{0:T(1024)}, f32[768]{0:T(1024)S(1)}, u32[]{:S(2)}) copy-start(f32[768]{0:T(1024)S(1)} %convert_element_type.111) | copy-start | bytes 9220
  76.2 70.0 %copy-start.47 = (f32[768]{0:T(1024)}, f32[768]{0:T(1024)S(1)}, u32[]{:S(2)}) copy-start(f32[768]{0:T(1024)S(1)} %convert_element_type.112) | copy-start | bytes 9220
  80.1 9.6 collective-permute-start.3
  89.8 28.8 %collective-permute-start.4 = (bf16[384,768]{1,0:T(8,128)(2,1)S(1)}, bf16[384,768]{1,0:T(8,128)(2,1)S(1)}, u32[]{:S(2)}, u32[]{:S(2)}) collective-permute-start(bf16[384,768]{1,0:T(8,128)(2,1)S(1)} %get-tuple-element.237), channel_id=1, source_target_pairs={{0,16},{1,17},{2,18},{3,19},{4,20},{5,21},{6,22},{7,23},{8,24},{9,... | collective-permute-start | bytes 1769480 | tf_op jit(solution)/shard_map/ppermute | solution.py:69
  92.4 26.3 %copy-start.37 = (f32[1058]{0:T(1024)}, f32[1058]{0:T(1024)S(1)}, u32[]{:S(2)}) copy-start(f32[1058]{0:T(1024)S(1)} %fusion.69) | copy-start | bytes 12700
  92.4 53.7 %copy-start.33 = (f32[1058]{0:T(1024)}, f32[1058]{0:T(1024)S(1)}, u32[]{:S(2)}) copy-start(f32[1058]{0:T(1024)S(1)} %fusion.73) | copy-start | bytes 12700
  235.9 118.6 %copy-start.4 = (f32[1058,768]{1,0:T(8,128)}, f32[1058,768]{1,0:T(8,128)S(1)}, u32[]{:S(2)}) copy-start(f32[1058,768]{1,0:T(8,128)S(1)} %get-tuple-element.248) | copy-start | bytes 9750532
  235.9 23.9 %copy-start.31 = (f32[768]{0:T(1024)S(1)}, f32[768]{0:T(1024)}, u32[]{:S(2)}) copy-start(f32[768]{0:T(1024)} %convert_element_type.122) | copy-start | bytes 9220
  235.9 23.9 %copy-start.39 = (f32[768]{0:T(1024)S(1)}, f32[768]{0:T(1024)}, u32[]{:S(2)}) copy-start(f32[768]{0:T(1024)} %convert_element_type.123) | copy-start | bytes 9220
  235.9 23.9 %copy-start.44 = (f32[3072]{0:T(1024)S(1)}, f32[3072]{0:T(1024)}, u32[]{:S(2)}) copy-start(f32[3072]{0:T(1024)} %convert_element_type.125) | copy-start | bytes 36868
  236.0 118.6 %copy-start.25 = (f32[1058]{0:T(1024)}, f32[1058]{0:T(1024)S(1)}, u32[]{:S(2)}) copy-start(f32[1058]{0:T(1024)S(1)} %broadcast_multiply_fusion) | copy-start | bytes 12700
  236.5 118.0 %copy-start.27 = (f32[1058]{0:T(1024)}, f32[1058]{0:T(1024)S(1)}, u32[]{:S(2)}) copy-start(f32[1058]{0:T(1024)S(1)} %fusion.74) | copy-start | bytes 12700
  361.5 249.4 %reduce-scatter.11.cloned.1.call-start = ((), (), s32[]{:S(2)}) async-start(), calls=%async_computation.13 | async-start | bytes 2433024 | tf_op jit(solution)/shard_map/reduce_scatter | solution.py:116
  398.2 11.7 %copy-start.3 = (bf16[2,529,12,64]{1,3,2,0:T(8,128)(2,1)S(1)}, bf16[2,529,12,64]{1,3,2,0:T(8,128)(2,1)}, u32[]{:S(2)}) copy-start(bf16[2,529,12,64]{1,3,2,0:T(8,128)(2,1)} %get-tuple-element.422) | copy-start | bytes 4875268 | tf_op jit(solution)/shard_map/while
  448.4 11.4 %copy-start.3 = (bf16[2,529,12,64]{1,3,2,0:T(8,128)(2,1)S(1)}, bf16[2,529,12,64]{1,3,2,0:T(8,128)(2,1)}, u32[]{:S(2)}) copy-start(bf16[2,529,12,64]{1,3,2,0:T(8,128)(2,1)} %get-tuple-element.422) | copy-start | bytes 4875268 | tf_op jit(solution)/shard_map/while
  489.1 202.7 %reduce-scatter.9.cloned.1.call-start = ((), (), s32[]{:S(2)}) async-start(), calls=%async_computation.12 | async-start | bytes 2433024 | tf_op jit(solution)/shard_map/reduce_scatter | solution.py:115
  501.9 294.4 %reduce-scatter.7.cloned.1.call-start = ((), (), s32[]{:S(2)}) async-start(), calls=%async_computation.11 | async-start | bytes 2433024 | tf_op jit(solution)/shard_map/reduce_scatter | solution.py:113
  514.4 423.8 %reduce-scatter.15.cloned.1.call-start = ((), (), s32[]{:S(2)}) async-start(), calls=%async_computation.15 | async-start | bytes 9732096 | tf_op jit(solution)/shard_map/reduce_scatter | solution.py:122
  526.6 553.3 %reduce-scatter.17.cloned.1.call-start = ((), (), s32[]{:S(2)}) async-start(), calls=%async_computation.16 | async-start | bytes 9732096 | tf_op jit(solution)/shard_map/reduce_scatter | solution.py:124
  (46 other events, 239.5 us)
Sparse Core Ops, SparseCore 0:
  10.9 56.8 all-gather.7
  70.8 68.0 all-gather.5
  141.7 52.7 all-gather.9
  197.3 62.5 all-gather.11
  262.6 61.9 all-gather.13
  361.6 97.9 reduce-scatter.12
  489.2 97.9 reduce-scatter.10
  593.1 98.6 reduce-scatter.8
  697.6 98.6 reduce-scatter.6
  802.7 135.4 reduce-scatter.14
  944.7 135.1 reduce-scatter.16
